TPU v7x, 128 devices: a whole 4x4x4 slice. The times are simulated.
128 devices in a mesh: rep: 4 (over y_hi, core), dp: 32 (over y_lo, z, x).
Axes of the slice: x: 4, y: 4 (y_hi: 2, y_lo: 2; y = y_hi * 2 + y_lo), z: 4, core: 2. Of those that a mesh axis runs over, the one named last changes fastest.
Arguments:
- query_states: bfloat16 [1024, 32, 768], P(('rep', 'dp')), may hold values from -12 to 12
- passage_states: bfloat16 [512, 180, 768], P(('rep', 'dp')), may hold values from -12 to 12
- query_lengths: int32 [1024], P(('rep', 'dp')), may hold values from 8 to 32, as said below
- passage_lengths: int32 [512], P(('rep', 'dp')), may hold values from 45 to 180, as said below
- passage_ids: int32 [512, 180], P(('rep', 'dp')), may hold values from 2 to 30521, as said below
- positives: int32 [1024], P(('rep', 'dp')), may hold values from 0 to 127, as said below
- up_weight: bfloat16 [768, 3072], replicated, may hold values from -0.21875 to 0.21875
- up_bias: float32 [3072], replicated, may hold values from -3 to 3
- down_weight: bfloat16 [3072, 768], replicated, may hold values from -0.109375 to 0.109375
- down_bias: float32 [768], replicated, may hold values from -3 to 3
- norm_gain: float32 [768], replicated, may hold values from 0.5 to 1.5
- norm_bias: float32 [768], replicated, may hold values from -2 to 2
- proj_weight: bfloat16 [768, 128], replicated, may hold values from -0.21875 to 0.21875
Outputs:
- mean_loss: float32 [], replicated
- passage_grad: float32 [512, 180, 128], P(('rep', 'dp'))
- proj_grad: float32 [768, 128], replicated
Inputs may be any that keep to these rules, and one draw needn't show every extreme that they name: `query_lengths`: every device holds a query with all 32 slots real. `passage_lengths`: every device holds a passage with all 180 slots real. `passage_ids`: slots 0 and 1 of every passage hold ids 101 and 2; ids 999 to 1066 are punctuation. `positives`: index of the positive passage among the 128 passages of the query's replica group, in the order of the devices.
All inputs are finite; a program needn't handle non-finite values.
Results may differ from a plain program's by a relative error of at most 0.0055.
Values may be sent and summed in bfloat16 or wider, within the bound.
A program may use at most 128 MiB of HBM per device.

v0:
```python
import math
import jax
import jax.numpy as jnp
from jax import lax
from jax.sharding import PartitionSpec as P

temper = 0.05
eps_norm = 1e-06
punct_low = 999
punct_high = 1067


def in_one_piece(arrays, axis, dim, along):
    widths = [math.prod(a.shape[along:]) for a in arrays]
    both = jnp.concatenate(
        [a.reshape(*a.shape[:along], w) for a, w in zip(arrays, widths)], axis=along
    )
    out = lax.all_gather(both, axis, axis=dim, tiled=True)
    blocks = jnp.split(out, [sum(widths[:k]) for k in range(1, len(widths))], axis=along)
    return tuple((b.reshape(*out.shape[:along], *a.shape[along:]) for a, b in zip(arrays, blocks)))


def in_blocks(array, dim, peers):
    before, after = (array.shape[:dim], array.shape[dim + 1 :])
    return jnp.moveaxis(array.reshape(*before, peers, -1, *after), dim, 0)


def summed_on_arrival(array, axis, dim):
    blocks = in_blocks(array, dim, lax.axis_size(axis))
    arrived = lax.all_to_all(blocks, axis, split_axis=0, concat_axis=0, tiled=True)
    return arrived.astype(jnp.float32).sum(axis=0)


def encode_rows(
    token_rows, up_weight, up_bias, down_weight, down_bias, norm_gain, norm_bias, proj_weight
):
    upward = jnp.dot(token_rows, up_weight, preferred_element_type=jnp.float32) + up_bias
    activated = jax.nn.gelu(upward, approximate=False).astype(jnp.bfloat16)
    residual = (
        token_rows.astype(jnp.float32)
        + jnp.dot(activated, down_weight, preferred_element_type=jnp.float32)
        + down_bias
    )
    average = jnp.mean(residual, -1, keepdims=True)
    centered = residual - average
    variance = jnp.mean(centered * centered, -1, keepdims=True)
    hidden = (centered * lax.rsqrt(variance + eps_norm) * norm_gain + norm_bias).astype(
        jnp.bfloat16
    )
    projected = jnp.dot(hidden, proj_weight, preferred_element_type=jnp.float32)
    inverse = lax.rsqrt(jnp.sum(projected * projected, -1, keepdims=True) + eps_norm)
    return (hidden, projected * inverse, inverse)


def token_scores(query_flat, query_keep, block_emb, block_keep, query_count):
    item_count, pass_len, embed_dim = block_emb.shape
    flat_block = block_emb.reshape(item_count * pass_len, embed_dim)
    similar = lax.dot_general(
        query_flat, flat_block, (((1,), (1,)), ((), ())), preferred_element_type=jnp.float32
    )
    weights = (
        jnp.exp(similar / temper).reshape(-1, item_count, pass_len)
        * block_keep.astype(jnp.float32)[None]
    )
    totals = jnp.sum(weights, -1)
    soft_max = temper * jnp.log(totals) * query_keep[:, None]
    scores = jnp.sum(soft_max.reshape(query_count, -1, item_count), 1)
    return (scores, weights, totals)


def token_grads(query_flat, query_keep, block_emb, weights, totals, dscore, query_count):
    item_count, pass_len, embed_dim = block_emb.shape
    factor = (dscore[:, None, :] * query_keep.reshape(query_count, -1)[:, :, None]).reshape(
        -1, item_count
    ) / totals
    sim_grad = (
        (weights * factor[:, :, None]).reshape(-1, item_count * pass_len).astype(jnp.bfloat16)
    )
    flat_block = block_emb.reshape(item_count * pass_len, embed_dim)
    passage_term = lax.dot_general(
        sim_grad, query_flat, (((0,), (0,)), ((), ())), preferred_element_type=jnp.float32
    )
    query_term = jnp.dot(sim_grad, flat_block, preferred_element_type=jnp.float32)
    return (passage_term.reshape(item_count, pass_len, embed_dim), query_term)


def cross_entropy(scores, positives):
    log_total = jnp.log(jnp.sum(jnp.exp(scores), 1))
    onehot = (jnp.arange(scores.shape[1], dtype=jnp.int32)[None, :] == positives[:, None]).astype(
        jnp.float32
    )
    loss_sum = jnp.sum(log_total - jnp.sum(scores * onehot, 1))
    dscore = jnp.exp(scores - log_total[:, None]) - onehot
    return (loss_sum, dscore)


def norm_backward(gradient, normed, inverse):
    return (inverse * (gradient - normed * jnp.sum(normed * gradient, -1, keepdims=True))).astype(
        jnp.bfloat16
    )


def per_device(
    query_states,
    passage_states,
    query_lengths,
    passage_lengths,
    passage_ids,
    positives,
    up_weight,
    up_bias,
    down_weight,
    down_bias,
    norm_gain,
    norm_bias,
    proj_weight,
):
    query_count, query_len, model_width = query_states.shape
    pass_count, pass_len, _ = passage_states.shape
    embed_dim = proj_weight.shape[1]
    token_rows = jnp.concatenate(
        [query_states.reshape(-1, model_width), passage_states.reshape(-1, model_width)], 0
    )
    hidden, normed, inverse = encode_rows(
        token_rows, up_weight, up_bias, down_weight, down_bias, norm_gain, norm_bias, proj_weight
    )
    boundary = query_count * query_len
    query_emb = normed[:boundary].astype(jnp.bfloat16)
    pass_emb = normed[boundary:].astype(jnp.bfloat16).reshape(pass_count, pass_len, embed_dim)
    query_keep = (
        (jnp.arange(query_len, dtype=jnp.int32)[None, :] < query_lengths[:, None])
        .astype(jnp.float32)
        .reshape(-1)
    )
    is_punct = (passage_ids >= punct_low) & (passage_ids < punct_high)
    pass_keep = (
        (jnp.arange(pass_len, dtype=jnp.int32)[None, :] < passage_lengths[:, None])
        & jnp.logical_not(is_punct)
    ).astype(jnp.bfloat16)
    groups = lax.axis_size("dp")
    query_shaped = query_emb.reshape(query_count, query_len, embed_dim)
    keep_shaped = query_keep.astype(jnp.bfloat16).reshape(query_count, query_len)
    gathered, gathered_keep = in_one_piece((query_shaped, keep_shaped), "dp", 0, 2)
    group_query = query_count * groups
    block_query = math.gcd(group_query, 16)
    block_count = group_query // block_query
    query_blocks = gathered.reshape(block_count, block_query * query_len, embed_dim)
    keep_blocks = gathered_keep.astype(jnp.float32).reshape(block_count, block_query * query_len)

    def forward(paired):
        scores, _, _ = token_scores(paired[0], paired[1], pass_emb, pass_keep, block_query)
        return scores

    scores = lax.map(forward, (query_blocks, keep_blocks)).reshape(group_query, pass_count)
    owned_rows = lax.all_to_all(scores, "dp", split_axis=0, concat_axis=1, tiled=True)
    loss_sum, dscore = cross_entropy(owned_rows, positives)
    returned = lax.all_to_all(dscore, "dp", split_axis=1, concat_axis=0, tiled=True)
    grad_blocks = returned.reshape(block_count, block_query, pass_count)

    def backward(pass_grad, triple):
        block_emb, block_keep, block_grad = triple
        _, weights, totals = token_scores(block_emb, block_keep, pass_emb, pass_keep, block_query)
        passage_term, query_term = token_grads(
            block_emb, block_keep, pass_emb, weights, totals, block_grad, block_query
        )
        return (pass_grad + passage_term, query_term)

    start_grad = jnp.zeros((pass_count, pass_len, embed_dim), jnp.float32)
    passage_grad, query_terms = lax.scan(
        backward, start_grad, (query_blocks, keep_blocks, grad_blocks)
    )
    query_grad = summed_on_arrival(
        query_terms.reshape(group_query, query_len, embed_dim).astype(jnp.bfloat16), "dp", 0
    )
    query_grad = query_grad.reshape(query_count * query_len, embed_dim)
    query_back = norm_backward(query_grad, normed[:boundary], inverse[:boundary])
    pass_back = norm_backward(
        passage_grad.reshape(-1, embed_dim), normed[boundary:], inverse[boundary:]
    )
    all_back = jnp.concatenate([query_back, pass_back], 0)
    local_sum = lax.dot_general(
        hidden, all_back, (((0,), (0,)), ((), ())), preferred_element_type=jnp.float32
    )
    proj_total, loss_total = lax.psum((local_sum, loss_sum), ("rep", "dp"))
    mean_loss = loss_total / (query_count * lax.axis_size("rep") * groups)
    return (mean_loss, passage_grad, proj_total)


def solution(mesh):
    in_specs = (
        P(("rep", "dp"), None, None),
        P(("rep", "dp"), None, None),
        P(("rep", "dp")),
        P(("rep", "dp")),
        P(("rep", "dp"), None),
        P(("rep", "dp")),
        P(),
        P(),
        P(),
        P(),
        P(),
        P(),
        P(),
    )
    out_specs = (P(), P(("rep", "dp"), None, None), P())
    return jax.shard_map(
        per_device, mesh=mesh, in_specs=in_specs, out_specs=out_specs, check_vma=False
    )
```

profile of v0, /device:TPU:1, one launch (start us, length us, event | category | flops | bytes accessed | tf_op | source)
XLA Modules:
  0.0 595.7 jit_solution(12372179383174552325)
XLA Ops:
  7.2 1.4 copy.36
  9.8 39.0 %fusion.79 = (f32[976]{0:T(1024)S(1)}, f32[976,768]{1,0:T(8,128)S(1)}) fusion(f32[768]{0:T(1024)} %param.26, bf16[3072,768]{1,0:T(8,128)(2,1)} %param.25, f32[3072]{0:T(1024)} %param.24, bf16[768,3072]{1,0:T(8,128)(2,1)} %param.23, bf16[720,768]{1,0:T(8,128)(2,1)} %reshape.220, bf16[256,768]{1,0:T(8,128)(2,1)} %bitcast.103), kind=kOutput, calls=%fused_computation.118 | convolution fusion | flops 9416821760 | bytes 13953856 | tf_op jit(solution)/shard_map/dot_general | solution.py:41
  53.0 139.8 %all-gather.2.cloned.1.call-done = bf16[256,32,129]{2,1,0:T(8,128)(2,1)} async-done(((bf16[8,32,129]{2,1,0:T(8,128)(2,1)}), bf16[256,32,129]{2,1,0:T(8,128)(2,1)}) %all-gather.2.cloned.1.call-update) | async-done | bytes 2113552 | tf_op jit(solution)/shard_map/all_gather | solution.py:18
  192.8 2.7 convert_reduce_fusion
  195.6 3.3 split.8
  198.9 31.5 %while.23 = (s32[]{:T(128)}, f32[16,16,4]{1,0,2:T(8,128)S(1)}, bf16[16,512,128]{2,1,0:T(8,128)(2,1)}, bf16[720,128]{1,0:T(8,128)(2,1)S(1)}, bf16[4,180]{1,0:T(4,...) while((s32[]{:T(128)}, f32[16,16,4]{1,0,2:T(8,128)S(1)}, bf16[16,512,128]{2,1,0:T(8,128)(2,1)}, ...), condition=%wide.region_6.7_spmd, body=%wide.region_3.6_spmd.sunk | while | flops 95480976 | bytes 6281597 | solution.py:154
  198.9 1.3 multiply_exponential_fusion.4
  200.9 1.3 multiply_exponential_fusion.4
  202.9 1.3 multiply_exponential_fusion.4
  204.8 1.3 multiply_exponential_fusion.4
  206.8 1.3 multiply_exponential_fusion.4
  208.8 1.3 multiply_exponential_fusion.4
  210.8 1.3 multiply_exponential_fusion.4
  212.7 1.3 multiply_exponential_fusion.4
  214.7 1.3 multiply_exponential_fusion.4
  216.7 1.3 multiply_exponential_fusion.4
  218.6 1.3 multiply_exponential_fusion.4
  222.6 1.3 multiply_exponential_fusion.4
  224.5 1.3 multiply_exponential_fusion.4
  228.5 1.3 multiply_exponential_fusion.4
  231.2 6.2 %all-to-all-start = ((f32[32,8,4]{1,2,0:T(4,128)}), f32[32,8,4]{1,2,0:T(4,128)S(1)}, u32[]{:S(2)}, u32[]{:S(2)}) async-start(f32[32,8,4]{1,2,0:T(4,128)} %copy.39), calls=%async_computation | async-start | bytes 131072 | tf_op jit(solution)/shard_map/all_to_all | solution.py:155
  237.4 7.2 %all-to-all-done = f32[32,8,4]{1,2,0:T(4,128)S(1)} async-done(((f32[32,8,4]{1,2,0:T(4,128)}), f32[32,8,4]{1,2,0:T(4,128)S(1)}, u32[]{:S(2)}, u32[]{:S(2)}) %all-to-all-start) | async-done | bytes 4128 | tf_op jit(solution)/shard_map/all_to_all | solution.py:155
  246.1 3.9 all-to-all-start.1
  249.9 7.2 %all-to-all-done.1 = f32[8,32,4]{0,2,1:T(4,128)S(1)} async-done(((f32[8,32,4]{0,2,1:T(4,128)}), f32[8,32,4]{0,2,1:T(4,128)S(1)}, u32[]{:S(2)}, u32[]{:S(2)}) %all-to-all-start.1) | async-done | bytes 4128 | tf_op jit(solution)/shard_map/all_to_all | solution.py:157
  257.2 134.8 %while.24 = (s32[]{:T(128)}, f32[4,180,128]{2,1,0:T(8,128)}, bf16[16,512,128]{2,1,0:T(8,128)(2,1)}, bf16[16,512,128]{2,1,0:T(8,128)(2,1)}, bf16[720,128]{1,0:T(8...) while((s32[]{:T(128)}, f32[4,180,128]{2,1,0:T(8,128)}, ...), condition=%wide.region_13.14_spmd.clone, body=%wide.region_11.13_spmd.clone.sunk | while | flops 285514432 | bytes 21625324 | solution.py:169
  260.6 1.7 multiply_convert_fusion.3
  263.5 1.3 convolution_add_fusion.2
  269.0 1.7 multiply_convert_fusion.3
  271.9 1.3 convolution_add_fusion.2
  277.4 1.7 multiply_convert_fusion.3
  280.3 1.3 convolution_add_fusion.2
  285.8 1.7 multiply_convert_fusion.3
  288.8 1.3 convolution_add_fusion.2
  294.2 1.7 multiply_convert_fusion.3
  297.2 1.3 convolution_add_fusion.2
  302.7 1.7 multiply_convert_fusion.3
  305.6 1.3 convolution_add_fusion.2
  311.1 1.7 multiply_convert_fusion.3
  314.0 1.3 convolution_add_fusion.2
  319.5 1.7 multiply_convert_fusion.3
  322.4 1.3 convolution_add_fusion.2
  327.9 1.7 multiply_convert_fusion.3
  330.9 1.3 convolution_add_fusion.2
  336.4 1.7 multiply_convert_fusion.3
  339.3 1.3 convolution_add_fusion.2
  344.8 1.7 multiply_convert_fusion.3
  347.7 1.3 convolution_add_fusion.2
  353.2 1.7 multiply_convert_fusion.3
  356.1 1.3 convolution_add_fusion.2
  361.6 1.7 multiply_convert_fusion.3
  364.6 1.3 convolution_add_fusion.2
  370.1 1.7 multiply_convert_fusion.3
  373.0 1.3 convolution_add_fusion.2
  378.5 1.7 multiply_convert_fusion.3
  381.4 1.3 convolution_add_fusion.2
  386.9 1.7 multiply_convert_fusion.3
  389.8 1.3 convolution_add_fusion.2
  392.0 4.9 all-to-all-start.2
  398.5 15.8 %all-to-all-done.2 = bf16[32,8,32,128]{3,2,1,0:T(8,128)(2,1)} async-done(((bf16[32,8,32,128]{3,2,1,0:T(8,128)(2,1)}), bf16[32,8,32,128]{3,2,1,0:T(8,128)(2,1)}, u32[]{:S(2)}, u32[]{:S(2)}) %all-to-all-start.2) | async-done | bytes 2097184 | tf_op jit(solution)/shard_map/all_to_all | solution.py:30
  414.3 1.9 convert_reduce_fusion.1
  416.5 1.4 fusion.32
  417.9 87.4 %psum.14 = f32[]{:T(128)} all-reduce(f32[]{:T(128)} %get-tuple-element.186), channel_id=1, replica_groups=mesh['rep'=4,'dp'=32] {'rep','dp'}, use_global_device_ids=true, to_apply=%region_10.11 | all-reduce | flops 1 | bytes 8 | tf_op jit(solution)/shard_map/psum | solution.py:184
  506.7 79.2 %all-reduce.2.cloned.1.call-done = f32[768,128]{1,0:T(8,128)} async-done(((f32[768,128]{1,0:T(8,128)}), f32[768,128]{1,0:T(8,128)}) %all-reduce.2.cloned.1.call-update) | async-done | bytes 393232 | tf_op jit(solution)/shard_map/psum | solution.py:184
  586.0 1.8 copy.73
  (499 shorter events, 107.7 us)
Async XLA Ops:
  7.2 43.9 %copy-start = (bf16[768,128]{1,0:T(8,128)(2,1)S(1)}, bf16[768,128]{1,0:T(8,128)(2,1)}, u32[]{:S(2)}) copy-start(bf16[768,128]{1,0:T(8,128)(2,1)} %param.29) | copy-start | bytes 589828
  7.2 185.6 %all-gather.2.cloned.1.call-start = ((), (), s32[]{:S(2)}) async-start(), calls=%async_computation.3 | async-start | bytes 4325376 | tf_op jit(solution)/shard_map/all_gather | solution.py:18
  9.7 39.6 %copy-start.10 = (f32[768]{0:T(1024)S(1)}, f32[768]{0:T(1024)}, u32[]{:S(2)}) copy-start(f32[768]{0:T(1024)} %param.28) | copy-start | bytes 9220
  9.8 39.6 %copy-start.11 = (f32[768]{0:T(1024)S(1)}, f32[768]{0:T(1024)}, u32[]{:S(2)}) copy-start(f32[768]{0:T(1024)} %param.27) | copy-start | bytes 9220
  48.8 3.1 copy-start.13
  49.3 3.6 copy-start.9
  49.3 3.6 copy-start.14
  49.9 1.1 copy-start.4
  51.7 345.2 %copy-start.8 = (f32[976]{0:T(1024)}, f32[976]{0:T(1024)S(1)}, u32[]{:S(2)}) copy-start(f32[976]{0:T(1024)S(1)} %add_rsqrt_fusion) | copy-start | bytes 11716
  51.9 147.0 %copy-start.6 = (f32[976,128]{1,0:T(8,128)}, f32[976,128]{1,0:T(8,128)S(1)}, u32[]{:S(2)}) copy-start(f32[976,128]{1,0:T(8,128)S(1)} %broadcast_multiply_fusion) | copy-start | bytes 1499140
  198.9 45.7 %copy-start.12 = (s32[8]{0:T(128)S(1)}, s32[8]{0:T(128)}, u32[]{:S(2)}) copy-start(s32[8]{0:T(128)} %param.22) | copy-start | bytes 100
  231.2 13.4 %all-to-all-start = ((f32[32,8,4]{1,2,0:T(4,128)}), f32[32,8,4]{1,2,0:T(4,128)S(1)}, u32[]{:S(2)}, u32[]{:S(2)}) async-start(f32[32,8,4]{1,2,0:T(4,128)} %copy.39), calls=%async_computation | async-start | bytes 131072 | tf_op jit(solution)/shard_map/all_to_all | solution.py:155
  246.1 11.0 %all-to-all-start.1 = ((f32[8,32,4]{0,2,1:T(4,128)}), f32[8,32,4]{0,2,1:T(4,128)S(1)}, u32[]{:S(2)}, u32[]{:S(2)}) async-start(f32[8,32,4]{0,2,1:T(4,128)} %fusion.40), calls=%async_computation.1 | async-start | bytes 131072 | tf_op jit(solution)/shard_map/all_to_all | solution.py:157
  260.5 3.0 copy-start.1
  264.8 0.8 copy-start.2
  268.9 3.0 copy-start.1
  273.2 0.8 copy-start.2
  277.3 3.0 copy-start.1
  281.7 0.8 copy-start.2
  285.7 3.0 copy-start.1
  290.1 0.8 copy-start.2
  294.2 3.0 copy-start.1
  298.5 0.8 copy-start.2
  302.6 3.0 copy-start.1
  306.9 0.8 copy-start.2
  311.0 3.0 copy-start.1
  315.3 0.8 copy-start.2
  319.4 3.0 copy-start.1
  323.8 0.8 copy-start.2
  327.8 3.0 copy-start.1
  332.2 0.8 copy-start.2
  336.3 3.0 copy-start.1
  340.6 0.8 copy-start.2
  344.7 3.0 copy-start.1
  349.1 0.8 copy-start.2
  353.1 3.0 copy-start.1
  357.5 0.8 copy-start.2
  361.6 3.0 copy-start.1
  365.9 0.8 copy-start.2
  370.0 3.0 copy-start.1
  374.3 0.8 copy-start.2
  378.4 3.0 copy-start.1
  382.7 0.8 copy-start.2
  386.8 3.0 copy-start.1
  391.2 0.8 copy-start.2
  392.0 6.1 %copy-start.7 = (f32[976,128]{1,0:T(8,128)S(1)}, f32[976,128]{1,0:T(8,128)}, u32[]{:S(2)}) copy-start(f32[976,128]{1,0:T(8,128)} %copy-done.6) | copy-start | bytes 1499140
  392.0 24.5 %copy-start.5 = (bf16[976,768]{1,0:T(8,128)(2,1)S(1)}, bf16[976,768]{1,0:T(8,128)(2,1)}, u32[]{:S(2)}) copy-start(bf16[976,768]{1,0:T(8,128)(2,1)} %copy-done.4) | copy-start | bytes 4497412
  392.0 22.3 %all-to-all-start.2 = ((bf16[32,8,32,128]{3,2,1,0:T(8,128)(2,1)}), bf16[32,8,32,128]{3,2,1,0:T(8,128)(2,1)}, u32[]{:S(2)}, u32[]{:S(2)}) async-start(bf16[32,8,32,128]{3,2,1,0:T(8,128)(2,1)} %bitcast.97), calls=%async_computation.2 | async-start | bytes 4194304 | tf_op jit(solution)/shard_map/all_to_all | solution.py:30
  396.9 109.0 %copy-start.3 = (f32[4,180,128]{2,1,0:T(8,128)S(1)}, f32[4,180,128]{2,1,0:T(8,128)}, u32[]{:S(2)}) copy-start(f32[4,180,128]{2,1,0:T(8,128)} %get-tuple-element.153) | copy-start | bytes 1105924
  396.9 189.1 %all-reduce.2.cloned.1.call-start = ((), (), s32[]{:S(2)}) async-start(), calls=%async_computation.4 | async-start | bytes 786432 | tf_op jit(solution)/shard_map/psum | solution.py:184
  396.9 19.4 %slice-start = ((f32[976]{0:T(1024)}), f32[256]{0:T(256)S(1)}, s32[]{:S(2)}) async-start(f32[976]{0:T(1024)} %copy-done.8), calls=%async_computation.5 | async-start | bytes 2048 | tf_op jit(solution)/shard_map/slice | solution.py:176
Sparse Core Ops, SparseCore 0:
  53.0 139.7 all-gather.1
  418.0 167.9 all-reduce.1
where the time goes:
time: 598 us; the launch traced here: 596 us
  waiting for transfers between devices  249 us (42%)
  matrix products  120 us (20%)
  blocking collectives  87.4 us (15%)
  local copies, waits for them, and re-layouts  61.1 us (10%)
  other arithmetic  44.3 us (7%)
  between operations  16.1 us (3%)
  starting transfers between devices  15 us (3%)
    all_gather x1, waiting for transfers between devices, in_one_piece(): out = lax.all_gather(both, axis, axis=dim, tiled=True)  140 us
    psum x1, blocking collectives, per_device(): proj_total, loss_total = lax.psum((local_sum, loss_sum), ('rep', 'dp'))  87.4 us
    psum x1, waiting for transfers between devices, per_device(): proj_total, loss_total = lax.psum((local_sum, loss_sum), ('rep', 'dp'))  79.2 us
    dot_general x32, matrix products, token_scores(): lax.dot_general(query_flat, flat_block, (((1,), (1,)), ((), ())), preferr...  40.4 us
    dot_general x1, matrix products, encode_rows(): jnp.dot(activated, down_weight, preferred_element_type=jnp.float32)  39 us
    convert_element_type x16, other arithmetic, token_grads(): (weights * factor[:, :, None]).reshape(-1, item_count * pass_len)  27.2 us
    mul x32, local copies, waits for them, and re-layouts, token_grads(): weights * factor[:, :, None]  23 us
    dot_general x16, matrix products, token_grads(): lax.dot_general(sim_grad, query_flat, (((0,), (0,)), ((), ())), preferred...  21.4 us
  transfers between devices with their start and end apart: 5, of which 5 were waited for; matrix products, arithmetic and copies ran while one was open for 0% of the time, Pallas kernels for 0%

commit v1 on v0

--- a/solution.py
+++ b/solution.py
@@ -3,6 +3,7 @@
 import jax.numpy as jnp
 from jax import lax
 from jax.sharding import PartitionSpec as P
+from jax.lax import psum
 
 temper = 0.05
 eps_norm = 1e-06
@@ -181,7 +182,12 @@
     local_sum = lax.dot_general(
         hidden, all_back, (((0,), (0,)), ((), ())), preferred_element_type=jnp.float32
     )
-    proj_total, loss_total = lax.psum((local_sum, loss_sum), ("rep", "dp"))
+    change_halves_in = lambda local, group_axis, device_axis: psum(
+        psum(local, group_axis), axis_name=device_axis
+    )
+    proj_total, loss_total = change_halves_in(
+        (local_sum, loss_sum), group_axis="dp", device_axis="rep"
+    )
     mean_loss = loss_total / (query_count * lax.axis_size("rep") * groups)
     return (mean_loss, passage_grad, proj_total)
 

time: 598 us -> 838 us (1.40)
  waiting for transfers between devices: 249 us -> 470 us
  blocking collectives: 87.4 us -> 107 us
    psum x1 -> x2, waiting for transfers between devices: 79.2 us -> 300 us  [the longest x1 300 us: per_device(): psum(local, group_axis)]
    psum x1 -> x2, blocking collectives: 87.4 us -> 107 us  [the longest x1 66.6 us: per_device(): psum(local, group_axis)]
  transfers between devices with their start and end apart: 5 -> 6, of which waited for: 5 -> 5; matrix products, arithmetic and copies ran while one was open for 0% -> 0% of each run, Pallas kernels for 0% -> 0%
where the time goes in v1:
time: 838 us; the launch traced here: 834 us
  waiting for transfers between devices  470 us (56%)
  matrix products  120 us (14%)
  blocking collectives  107 us (13%)
  local copies, waits for them, and re-layouts  61.1 us (7%)
  other arithmetic  42.9 us (5%)
  between operations  15.9 us (2%)
  starting transfers between devices  15.1 us (2%)
    psum x1, waiting for transfers between devices, per_device(): psum(local, group_axis)  300 us
    all_gather x1, waiting for transfers between devices, in_one_piece(): out = lax.all_gather(both, axis, axis=dim, tiled=True)  140 us
    psum x1, blocking collectives, per_device(): psum(local, group_axis)  66.6 us
    dot_general x32, matrix products, token_scores(): lax.dot_general(query_flat, flat_block, (((1,), (1,)), ((), ())), preferr...  40.4 us
    psum x1, blocking collectives, per_device(): psum(psum(local, group_axis), axis_name=device_axis)  40.1 us
    dot_general x1, matrix products, encode_rows(): jnp.dot(activated, down_weight, preferred_element_type=jnp.float32)  39 us
    convert_element_type x16, other arithmetic, token_grads(): (weights * factor[:, :, None]).reshape(-1, item_count * pass_len)  25.8 us
    mul x32, local copies, waits for them, and re-layouts, token_grads(): weights * factor[:, :, None]  23 us
  transfers between devices with their start and end apart: 6, of which 5 were waited for; matrix products, arithmetic and copies ran while one was open for 0% of the time, Pallas kernels for 0%

profile of v1, /device:TPU:1, one launch (start us, length us, event | category | flops | bytes accessed | tf_op | source)
XLA Modules:
  0.0 834.4 jit_solution(11840823748585069281)
XLA Ops:
  7.2 1.4 copy.36
  9.8 39.0 %fusion.79 = (f32[976]{0:T(1024)S(1)}, f32[976,768]{1,0:T(8,128)S(1)}) fusion(f32[768]{0:T(1024)} %param.26, bf16[3072,768]{1,0:T(8,128)(2,1)} %param.25, f32[3072]{0:T(1024)} %param.24, bf16[768,3072]{1,0:T(8,128)(2,1)} %param.23, bf16[720,768]{1,0:T(8,128)(2,1)} %reshape.220, bf16[256,768]{1,0:T(8,128)(2,1)} %bitcast.103), kind=kOutput, calls=%fused_computation.118 | convolution fusion | flops 9416821760 | bytes 13953856 | tf_op jit(solution)/shard_map/dot_general | solution.py:42
  53.0 139.8 %all-gather.2.cloned.1.call-done = bf16[256,32,129]{2,1,0:T(8,128)(2,1)} async-done(((bf16[8,32,129]{2,1,0:T(8,128)(2,1)}), bf16[256,32,129]{2,1,0:T(8,128)(2,1)}) %all-gather.2.cloned.1.call-update) | async-done | bytes 2113552 | tf_op jit(solution)/shard_map/all_gather | solution.py:19
  192.7 2.7 convert_reduce_fusion
  195.6 3.3 split.8
  198.9 31.5 %while.23 = (s32[]{:T(128)}, f32[16,16,4]{1,0,2:T(8,128)S(1)}, bf16[16,512,128]{2,1,0:T(8,128)(2,1)}, bf16[720,128]{1,0:T(8,128)(2,1)S(1)}, bf16[4,180]{1,0:T(4,...) while((s32[]{:T(128)}, f32[16,16,4]{1,0,2:T(8,128)S(1)}, bf16[16,512,128]{2,1,0:T(8,128)(2,1)}, ...), condition=%wide.region_6.7_spmd, body=%wide.region_3.6_spmd.sunk | while | flops 95480976 | bytes 6281597 | solution.py:155
  198.9 1.3 multiply_exponential_fusion.4
  200.8 1.3 multiply_exponential_fusion.4
  202.8 1.3 multiply_exponential_fusion.4
  204.8 1.3 multiply_exponential_fusion.4
  206.8 1.3 multiply_exponential_fusion.4
  208.7 1.3 multiply_exponential_fusion.4
  210.7 1.3 multiply_exponential_fusion.4
  212.7 1.3 multiply_exponential_fusion.4
  214.6 1.3 multiply_exponential_fusion.4
  218.6 1.3 multiply_exponential_fusion.4
  220.5 1.3 multiply_exponential_fusion.4
  224.5 1.3 multiply_exponential_fusion.4
  226.5 1.3 multiply_exponential_fusion.4
  231.1 6.2 all-to-all-start
  237.4 7.2 all-to-all-done
  246.0 3.9 all-to-all-start.1
  249.9 7.2 all-to-all-done.1
  257.1 133.4 %while.24 = (s32[]{:T(128)}, f32[4,180,128]{2,1,0:T(8,128)}, bf16[16,512,128]{2,1,0:T(8,128)(2,1)}, bf16[16,512,128]{2,1,0:T(8,128)(2,1)}, bf16[720,128]{1,0:T(8...) while((s32[]{:T(128)}, f32[4,180,128]{2,1,0:T(8,128)}, ...), condition=%wide.region_14.15_spmd.clone, body=%wide.region_12.14_spmd.clone.sunk | while | flops 285514432 | bytes 21625324 | solution.py:170
  260.5 1.6 multiply_convert_fusion.3
  263.3 1.3 convolution_add_fusion.2
  268.8 1.6 multiply_convert_fusion.3
  271.7 1.3 convolution_add_fusion.2
  277.2 1.6 multiply_convert_fusion.3
  280.0 1.3 convolution_add_fusion.2
  285.5 1.6 multiply_convert_fusion.3
  288.4 1.3 convolution_add_fusion.2
  293.8 1.6 multiply_convert_fusion.3
  296.7 1.3 convolution_add_fusion.2
  302.2 1.6 multiply_convert_fusion.3
  305.0 1.3 convolution_add_fusion.2
  310.5 1.6 multiply_convert_fusion.3
  313.3 1.3 convolution_add_fusion.2
  318.8 1.6 multiply_convert_fusion.3
  321.7 1.3 convolution_add_fusion.2
  327.2 1.6 multiply_convert_fusion.3
  330.0 1.3 convolution_add_fusion.2
  335.5 1.6 multiply_convert_fusion.3
  338.4 1.3 convolution_add_fusion.2
  343.9 1.6 multiply_convert_fusion.3
  346.7 1.3 convolution_add_fusion.2
  352.2 1.6 multiply_convert_fusion.3
  355.0 1.3 convolution_add_fusion.2
  360.5 1.6 multiply_convert_fusion.3
  363.4 1.3 convolution_add_fusion.2
  368.9 1.6 multiply_convert_fusion.3
  371.7 1.3 convolution_add_fusion.2
  377.2 1.6 multiply_convert_fusion.3
  380.0 1.3 convolution_add_fusion.2
  385.5 1.6 multiply_convert_fusion.3
  388.4 1.3 convolution_add_fusion.2
  390.5 4.9 all-to-all-start.2
  397.0 15.8 %all-to-all-done.2 = bf16[32,8,32,128]{3,2,1,0:T(8,128)(2,1)} async-done(((bf16[32,8,32,128]{3,2,1,0:T(8,128)(2,1)}), bf16[32,8,32,128]{3,2,1,0:T(8,128)(2,1)}, u32[]{:S(2)}, u32[]{:S(2)}) %all-to-all-start.2) | async-done | bytes 2097184 | tf_op jit(solution)/shard_map/all_to_all | solution.py:31
  412.8 1.9 convert_reduce_fusion.1
  415.0 1.4 fusion.32
  416.5 300.3 %all-reduce.3.cloned.1.call-done = f32[768,128]{1,0:T(8,128)} async-done(((f32[768,128]{1,0:T(8,128)}), f32[768,128]{1,0:T(8,128)}) %all-reduce.3.cloned.1.call-update) | async-done | bytes 393232 | tf_op jit(solution)/shard_map/psum | solution.py:186
  716.8 66.6 %psum.28 = f32[]{:T(128)} all-reduce(f32[]{:T(128)} %get-tuple-element.186), channel_id=1, replica_groups=mesh['rep'=4,'dp'=32] {'dp'}, use_global_device_ids=true, to_apply=%region_10.11 | all-reduce | flops 1 | bytes 8 | tf_op jit(solution)/shard_map/psum | solution.py:186
  783.4 40.1 %psum.29 = f32[]{:T(128)} all-reduce(f32[]{:T(128)} %psum.28), channel_id=1, replica_groups=mesh['rep'=4,'dp'=32] {'rep'}, use_global_device_ids=true, to_apply=%region_11.12 | all-reduce | flops 1 | bytes 8 | tf_op jit(solution)/shard_map/psum | solution.py:185
  825.0 1.8 copy.74
  (503 shorter events, 109.1 us)
Async XLA Ops:
  7.2 43.8 %copy-start = (bf16[768,128]{1,0:T(8,128)(2,1)S(1)}, bf16[768,128]{1,0:T(8,128)(2,1)}, u32[]{:S(2)}) copy-start(bf16[768,128]{1,0:T(8,128)(2,1)} %param.29) | copy-start | bytes 589828
  7.2 185.5 %all-gather.2.cloned.1.call-start = ((), (), s32[]{:S(2)}) async-start(), calls=%async_computation.3 | async-start | bytes 4325376 | tf_op jit(solution)/shard_map/all_gather | solution.py:19
  9.7 39.6 %copy-start.10 = (f32[768]{0:T(1024)S(1)}, f32[768]{0:T(1024)}, u32[]{:S(2)}) copy-start(f32[768]{0:T(1024)} %param.28) | copy-start | bytes 9220
  9.8 39.6 %copy-start.11 = (f32[768]{0:T(1024)S(1)}, f32[768]{0:T(1024)}, u32[]{:S(2)}) copy-start(f32[768]{0:T(1024)} %param.27) | copy-start | bytes 9220
  48.8 3.1 copy-start.13
  49.3 3.6 copy-start.9
  49.3 3.6 copy-start.14
  49.9 1.1 copy-start.4
  51.7 343.8 %copy-start.8 = (f32[976]{0:T(1024)}, f32[976]{0:T(1024)S(1)}, u32[]{:S(2)}) copy-start(f32[976]{0:T(1024)S(1)} %add_rsqrt_fusion) | copy-start | bytes 11716
  51.9 147.0 %copy-start.6 = (f32[976,128]{1,0:T(8,128)}, f32[976,128]{1,0:T(8,128)S(1)}, u32[]{:S(2)}) copy-start(f32[976,128]{1,0:T(8,128)S(1)} %broadcast_multiply_fusion) | copy-start | bytes 1499140
  198.9 45.7 %copy-start.12 = (s32[8]{0:T(128)S(1)}, s32[8]{0:T(128)}, u32[]{:S(2)}) copy-start(s32[8]{0:T(128)} %param.22) | copy-start | bytes 100
  231.1 13.4 %all-to-all-start = ((f32[32,8,4]{1,2,0:T(4,128)}), f32[32,8,4]{1,2,0:T(4,128)S(1)}, u32[]{:S(2)}, u32[]{:S(2)}) async-start(f32[32,8,4]{1,2,0:T(4,128)} %copy.39), calls=%async_computation | async-start | bytes 131072 | tf_op jit(solution)/shard_map/all_to_all | solution.py:156
  246.0 11.0 %all-to-all-start.1 = ((f32[8,32,4]{0,2,1:T(4,128)}), f32[8,32,4]{0,2,1:T(4,128)S(1)}, u32[]{:S(2)}, u32[]{:S(2)}) async-start(f32[8,32,4]{0,2,1:T(4,128)} %fusion.40), calls=%async_computation.1 | async-start | bytes 131072 | tf_op jit(solution)/shard_map/all_to_all | solution.py:158
  260.4 2.9 copy-start.1
  264.7 0.8 copy-start.2
  268.7 2.9 copy-start.1
  273.0 0.8 copy-start.2
  277.1 2.9 copy-start.1
  281.4 0.8 copy-start.2
  285.4 2.9 copy-start.1
  289.7 0.8 copy-start.2
  293.8 2.9 copy-start.1
  298.0 0.8 copy-start.2
  302.1 2.9 copy-start.1
  306.3 0.8 copy-start.2
  310.4 2.9 copy-start.1
  314.7 0.8 copy-start.2
  318.7 2.9 copy-start.1
  323.0 0.8 copy-start.2
  327.1 2.9 copy-start.1
  331.4 0.8 copy-start.2
  335.4 2.9 copy-start.1
  339.7 0.8 copy-start.2
  343.8 2.9 copy-start.1
  348.0 0.8 copy-start.2
  352.1 2.9 copy-start.1
  356.4 0.8 copy-start.2
  360.4 2.9 copy-start.1
  364.7 0.8 copy-start.2
  368.8 2.9 copy-start.1
  373.0 0.8 copy-start.2
  377.1 2.9 copy-start.1
  381.4 0.8 copy-start.2
  385.4 2.9 copy-start.1
  389.7 0.8 copy-start.2
  390.5 6.1 copy-start.7
  390.5 24.5 %copy-start.5 = (bf16[976,768]{1,0:T(8,128)(2,1)S(1)}, bf16[976,768]{1,0:T(8,128)(2,1)}, u32[]{:S(2)}) copy-start(bf16[976,768]{1,0:T(8,128)(2,1)} %copy-done.4) | copy-start | bytes 4497412
  390.5 22.3 %all-to-all-start.2 = ((bf16[32,8,32,128]{3,2,1,0:T(8,128)(2,1)}), bf16[32,8,32,128]{3,2,1,0:T(8,128)(2,1)}, u32[]{:S(2)}, u32[]{:S(2)}) async-start(bf16[32,8,32,128]{3,2,1,0:T(8,128)(2,1)} %bitcast.97), calls=%async_computation.2 | async-start | bytes 4194304 | tf_op jit(solution)/shard_map/all_to_all | solution.py:31
  395.4 428.7 %copy-start.3 = (f32[4,180,128]{2,1,0:T(8,128)S(1)}, f32[4,180,128]{2,1,0:T(8,128)}, u32[]{:S(2)}) copy-start(f32[4,180,128]{2,1,0:T(8,128)} %get-tuple-element.153) | copy-start | bytes 1105924
  395.4 321.3 %all-reduce.3.cloned.1.call-start = ((), (), s32[]{:S(2)}) async-start(), calls=%async_computation.4 | async-start | bytes 786432 | tf_op jit(solution)/shard_map/psum | solution.py:186
  395.5 19.4 %slice-start = ((f32[976]{0:T(1024)}), f32[256]{0:T(256)S(1)}, s32[]{:S(2)}) async-start(f32[976]{0:T(1024)} %copy-done.8), calls=%async_computation.6 | async-start | bytes 2048 | tf_op jit(solution)/shard_map/slice | solution.py:177
  416.4 408.6 %all-reduce.5.cloned.1.call-start = ((), (), s32[]{:S(2)}) async-start(), calls=%async_computation.5 | async-start | bytes 786432 | tf_op jit(solution)/shard_map/psum | solution.py:185
Sparse Core Ops, SparseCore 0:
  53.0 139.7 all-gather.1
  416.5 300.1 all-reduce.2
  719.3 61.3 all-reduce.4
